TPU v7x, 32 devices: a 4x4x1 block of a 4x4x8 slice. The times are simulated.
32 devices in a mesh: pod: 1 (over z), data: 4 (over y), model: 8 (over x, core).
Axes of the slice: x: 4, y: 4, z: 1, core: 2. Of those that a mesh axis runs over, the one named last changes fastest.
The devices are a block of a 4x4x8 slice.
Arguments:
- x_in: bfloat16 [4, 1024, 2048], P(('pod', 'data'), 'model')
- dy_in: bfloat16 [4, 1024, 2048], P(('pod', 'data'), 'model')
- w_q: bfloat16 [2048, 16, 128], P(None, 'model')
- w_k: bfloat16 [1, 2048, 128], replicated
- w_v: bfloat16 [1, 2048, 128], replicated
- w_o: bfloat16 [16, 128, 2048], P('model')
Outputs:
- output 1: bfloat16 [4, 1024, 2048], P(('pod', 'data'), 'model')
- output 2: float32 [2048, 16, 128], P(('pod', 'data'), 'model')
- output 3: float32 [2048, 128], P(('pod', 'model', 'data'))
- output 4: float32 [2048, 128], P(('pod', 'model', 'data'))
- output 5: float32 [16, 128, 2048], P(('pod', 'model'), None, 'data')
All inputs are finite; a program needn't handle non-finite values.
Results may differ from a plain program's by a relative error of at most 0.00940278.
Values are sent between devices in bfloat16 or wider.
A program may use at most 768 MiB of HBM per device.

v0:
```python
import functools

import jax
import jax.numpy as jnp
from jax import lax
from jax.experimental import pallas as pl
from jax.experimental.pallas import tpu as pltpu
from jax.sharding import PartitionSpec as P

F32 = jnp.float32
BF16 = jnp.bfloat16
NN = (((1,), (0,)), ((), ()))
NT = (((1,), (1,)), ((), ()))
TN = (((0,), (0,)), ((), ()))


def dot(a, b, dims):
    return lax.dot_general(a, b, dims, preferred_element_type=F32)


def body(cfg, x_hbm, dy_hbm, wq_hbm, wo_hbm, wk_hbm, wv_hbm,
         dx_out, dwq_out, dwk_out, dwv_out, dwo_out,
         xf, yf, wqs, wo, wkv, wq2, wq2f, qf, kv, of, prob, dsf, dqf, dof, kvb, dqa,
         kvp, kvr, kr, dwa, yr, wkp, wkr, dxacc, dx_ref, dwq_ref, dwk_ref, dwv_ref, dwo_ref,
         load_sem, out_sem, ag_s, ag_r, wy_s, wy_r, wd_s, wd_r, dq_s, dq_r,
         kd_s, kd_r, kr_s, kr_r, yr_s, yr_r, wk_s, wk_r):
    tok, width, head_cols, head_dim, chips, rows = cfg
    half = tok // 2
    chunk = 2 * tok
    seq = chips * chunk
    heads = head_cols // head_dim
    wcol = width // (2 * rows)
    hcol = width // 2
    qrow = 5 * width // 32
    erow = rows * qrow
    brow = (width - erow) // 2
    scale = head_dim ** -0.5

    me = lax.axis_index('model')
    cx = me // 2
    cc = me % 2
    cp = 1 - cc
    xright = (cx + 1) % chips
    xleft = (cx + chips - 1) % chips
    xfar = (cx + 2) % chips
    my = lax.axis_index('data')
    yup = (my + 1) % rows
    ydn = (my + rows - 1) % rows
    yfar = (my + 2) % rows
    to_r = {'model': xright * 2 + cc}
    to_l = {'model': xleft * 2 + cc}
    to_p = {'model': cx * 2 + cp}
    to_u = {'data': yup}
    to_d = {'data': ydn}
    to_f = {'data': yfar}

    def rcopy(src, dst, ssem, rsem, dev):
        return pltpu.make_async_remote_copy(src_ref=src, dst_ref=dst, send_sem=ssem, recv_sem=rsem,
                                            device_id=dev, device_id_type=pl.DeviceIdType.MESH)

    def piece(arr, xc, core, h, base):
        r = pl.ds((xc * 2 + core) * tok + h * half, half)
        if arr == 0:
            return xf.at[r, :]
        if arr == 3:
            return kvb.at[r, :]
        slot = (xc + chips - base) % chips
        if arr == 4:
            return wqs.at[core, slot, pl.ds(my * qrow + h * (qrow // 2), qrow // 2), :]
        if arr >= 5:
            return wqs.at[core, slot, pl.ds(erow + (arr - 5) * brow + h * (brow // 2), brow // 2), :]
        return yf.at[r, pl.ds((arr - 1) * hcol, hcol)]

    def ag_slot(xc, base, h, cross):
        away = (xc + chips - base) % chips
        return 2 * chips - 2 + away if cross else 2 * away - 2 + h

    def ag_copy(arr, idx, xc, core, h, dev):
        base = {'r': xright, 'l': xleft, 'p': cx}[dev]
        return rcopy(piece(arr, xc, core, h, cx), piece(arr, xc, core, h, base), ag_s.at[arr],
                     ag_r.at[arr, ag_slot(xc, base, h, dev == 'p')], {'r': to_r, 'l': to_l, 'p': to_p}[dev])

    def ag_ring_first(arr):
        return [ag_copy(arr, 0, cx, cc, 0, 'r'), ag_copy(arr, 2, cx, cc, 1, 'l')]

    def ag_first(arr):
        return ag_ring_first(arr) + [ag_copy(arr, 4, cx, cc, 0, 'p'), ag_copy(arr, 5, cx, cc, 1, 'p')]

    def ag_second(arr):
        return [ag_copy(arr, 1, cx, cc, 1, 'r'), ag_copy(arr, 3, cx, cc, 0, 'l')]

    def ag_own(arr):
        return ag_first(arr) + ag_second(arr)

    def ag_relay(arr):
        return [ag_copy(arr, 6, xleft, cc, 0, 'r'), ag_copy(arr, 7, xright, cc, 1, 'l')]

    def ag_cross(arr, idx, xc, h):
        return ag_copy(arr, idx, xc, cc, h, 'p')

    def ag_wait(arr, xc, core, h):
        p = piece(arr, xc, core, h, cx)
        rcopy(p, p, ag_s.at[arr], ag_r.at[arr, ag_slot(xc, cx, h, False)], to_p).wait_recv()

    def ag_relays(arr):
        relays = ag_relay(arr)
        ag_wait(arr, xleft, cc, 0)
        relays[0].start()
        ag_wait(arr, xright, cc, 1)
        relays[1].start()

    def ag_stage1(arr):
        ag_relays(arr)
        ag_cross(arr, 8, xleft, 0).start()
        ag_cross(arr, 11, xright, 1).start()

    def ag_stage2(arr):
        ag_wait(arr, xright, cc, 0)
        ag_cross(arr, 10, xright, 0).start()
        ag_wait(arr, xleft, cc, 1)
        ag_cross(arr, 9, xleft, 1).start()

    def ag_stage3(arr):
        ag_wait(arr, xfar, cc, 0)
        ag_cross(arr, 12, xfar, 0).start()
        ag_wait(arr, xfar, cc, 1)
        ag_cross(arr, 13, xfar, 1).start()

    def ag_partner(arr, xc):
        r = pl.ds((xc * 2 + cp) * tok, tok)
        if arr == 0:
            p = xf.at[r, :]
        elif arr == 3:
            p = kvb.at[r, :]
        elif arr >= 5:
            p = wqs.at[cp, (xc + chips - cx) % chips, pl.ds(erow + (arr - 5) * brow, brow), :]
        else:
            p = yf.at[r, pl.ds((arr - 1) * hcol, hcol)]
        rcopy(p, p, ag_s.at[arr], ag_r.at[arr, ag_slot(xc, cx, 0, True)], to_p).wait_recv()

    def ag_sent(arr):
        r = pl.ds(0, 7 * tok)
        p = {0: xf.at[r, :], 1: yf.at[r, pl.ds(0, hcol)], 2: yf.at[r, pl.ds(0, hcol)], 3: kvb.at[r, :],
             4: wqs.at[0, 0, pl.ds(0, 3 * qrow), :], 5: wqs.at[:, 0, pl.ds(0, 7 * brow // 2), :],
             6: wqs.at[:, 0, pl.ds(0, 7 * brow // 2), :]}[arr]
        rcopy(p, p, ag_s.at[arr], ag_r.at[arr, 0], to_p).wait_send()

    def wy_copy(idx, q, h, dev):
        p = wqs.at[cc, pl.ds(1, chips - 1), pl.ds(q * qrow + h * (qrow // 2), qrow // 2), :]
        return rcopy(p, p, wy_s.at[0], wy_r.at[idx], dev)

    wy_own = [wy_copy(0, my, 0, to_u), wy_copy(1, my, 1, to_d), wy_copy(2, my, 1, to_u), wy_copy(2, my, 0, to_d)]
    wy_relay = [wy_copy(2, ydn, 0, to_u), wy_copy(2, yup, 1, to_d)]

    def wy_pass():
        wy_copy(0, ydn, 0, to_u).wait_recv()
        wy_relay[0].start()
        wy_copy(1, yup, 1, to_u).wait_recv()
        wy_relay[1].start()

    def wy_total(count):
        p = wqs.at[cc, pl.ds(1, chips - 1), pl.ds(0, count * (qrow // 2)), :]
        return rcopy(p, p, wy_s.at[0], wy_r.at[2], to_u)

    wd_own = rcopy(wqs.at[cc, 0, pl.ds(0, erow), :], wqs.at[cc, 0, pl.ds(0, erow), :], wd_s.at[0], wd_r.at[0], to_p)
    wd_rest = rcopy(wqs.at[cc, pl.ds(1, chips - 1), pl.ds(0, erow), :], wqs.at[cc, pl.ds(1, chips - 1), pl.ds(0, erow), :],
                    wd_s.at[1], wd_r.at[1], to_p)

    def wy_end():
        wy_total(4).wait_recv()
        wd_rest.start()

    def dq_copy(xc, core):
        return rcopy(dqf.at[pl.ds((xc * 2 + core) * tok, tok), :], dqa.at[(cx + chips - xc) % chips, cc],
                     dq_s.at[0], dq_r.at[0], {'model': xc * 2 + core})

    dq_total = rcopy(dqf.at[pl.ds(0, 7 * tok), :], dqf.at[pl.ds(0, 7 * tok), :], dq_s.at[0], dq_r.at[0], to_p)

    def kd_copy(xc):
        return rcopy(kvp.at[xc * 2 + cp], kvr.at[xc], kd_s.at[0], kd_r.at[0], to_p)

    kd_total = rcopy(kvr, kvr, kd_s.at[0], kd_r.at[0], to_p)

    def kpart(xc, h):
        return kvp.at[xc * 2 + cc, pl.ds(h * half, half), :]

    def ring_src(kind, side):
        if kind == 0:
            return (xright, 1) if side == 0 else (xleft, 0)
        if kind == 1:
            return (xfar, 0) if side == 0 else (xfar, 1)
        return (xright, 0) if side == 0 else (xleft, 1)

    def k_copy(side, kind):
        xc, h = ring_src(kind, side)
        return rcopy(kpart(xc, h), kr.at[side, kind], kr_s.at[0], kr_r.at[side if kind == 1 else 2],
                     to_r if side == 0 else to_l)

    def k_pass():
        for side in range(2):
            k_copy(side, 1).wait_recv()
            xc, h = ring_src(2, side)
            ref = kpart(xc, h)
            ref[...] = ref[...] + kr[side, 1]
            k_copy(side, 2).start()

    order = ((yfar, 0), (yfar, 1), (yup, 1), (ydn, 0), (yup, 0), (ydn, 1), (my, 0), (my, 1))

    def y_blk(w, kind, side):
        pos = {(1, 0): 0, (1, 1): 1, (0, 0): 2, (0, 1): 3, (2, 0): 4, (2, 1): 5, (3, 0): 6, (3, 1): 7}[kind, side]
        if w == 0:
            return pos
        return order[pos][0] * 2 + order[pos][1]

    def y_copy(w, side, kind):
        return rcopy(dwa.at[w, y_blk(w, kind, side)], yr.at[w, side, kind], yr_s.at[0], yr_r.at[w, side if kind == 1 else 2],
                     to_u if side == 0 else to_d)

    def dw_block(w, kind, side):
        blk = y_blk(w, kind, side)
        if w == 0:
            dwa[0, blk] = dot(of[...], yf[:, blk * wcol:(blk + 1) * wcol], TN)
        else:
            dwa[1, blk] = dot(dqf[...], xf[:, pl.ds(pl.multiple_of(blk * wcol, wcol), wcol)], TN)

    def y_first(w, kind):
        for side in range(2):
            dw_block(w, kind, side)
            y_copy(w, side, kind).start()

    def dw_blocks(w, kind):
        for side in range(2):
            dw_block(w, kind, side)

    def y_pass(w):
        for side in range(2):
            y_copy(w, side, 1).wait_recv()
            blk = y_blk(w, 2, side)
            dwa[w, blk] = dwa[w, blk] + yr[w, side, 1]
            y_copy(w, side, 2).start()

    def y_final(w):
        p = yr.at[w, :, pl.ds(0, 2)]
        rcopy(p, p, yr_s.at[0], yr_r.at[w, 2], to_u).wait_recv()
        first = dwa[w, y_blk(w, 3, 0)] + yr[w, 1, 0] + yr[w, 0, 2]
        second = dwa[w, y_blk(w, 3, 1)] + yr[w, 0, 0] + yr[w, 1, 2]
        return first, second

    own_rows = pl.ds(me * tok, tok)
    loads = [pltpu.make_async_copy(x_hbm, xf.at[own_rows, :], load_sem.at[0]),
             pltpu.make_async_copy(wq_hbm, wq2, load_sem.at[1]),
             pltpu.make_async_copy(wk_hbm, wkv.at[:, pl.ds(0, head_dim)], load_sem.at[2]),
             pltpu.make_async_copy(wv_hbm, wkv.at[:, pl.ds(head_dim, head_dim)], load_sem.at[2])]
    for pos, (dest, part) in enumerate(order):
        src = pl.ds(pl.multiple_of((dest * 2 + part) * wcol, wcol), wcol)
        dst = pl.ds(pos * wcol, wcol)
        loads.append(pltpu.make_async_copy(dy_hbm.at[:, src], yf.at[own_rows, dst], load_sem.at[3]))
        loads.append(pltpu.make_async_copy(wo_hbm.at[:, src], wo.at[:, dst], load_sem.at[4]))
    for cp_ in loads:
        cp_.start()
    barrier = pltpu.get_barrier_semaphore()
    peers = [{'model': (me + k) % (2 * chips)} for k in range(1, 2 * chips)]
    for dev in peers + [to_u, to_d, to_f]:
        pl.semaphore_signal(barrier, inc=1, device_id=dev, device_id_type=pl.DeviceIdType.MESH)
    with jax.named_scope('barrier'):
        pl.semaphore_wait(barrier, 2 * chips + 2)
    loads[0].wait()
    for cp_ in ag_first(0):
        cp_.start()
    with jax.named_scope('loadw'):
        loads[1].wait()
        for k, ref in ((2, wkv), (3, yf.at[own_rows, :]), (4, wo)):
            pltpu.make_async_copy(ref, ref, load_sem.at[k]).wait()
        step = 2 * width // 8

        @pl.loop(0, 8)
        def _(b):
            r2 = pl.ds(pl.multiple_of(b * step, step), step)
            wq2f[r2, :] = wq2[r2, :].astype(F32)
            r1 = pl.ds(pl.multiple_of(b * (step // 2), step // 2), step // 2)
            for h in range(heads):
                wqs[cc, 0, r1, h * head_dim:(h + 1) * head_dim] = wq2f[pl.ds(b * step + h, step // 2, stride=heads), :].astype(BF16)

    for cp_ in ag_ring_first(4) + ag_second(4) + ag_second(0):
        cp_.start()
    wd_own.start()

    def chunk_of(s):
        return (cx + s + s // 2 - 2 * (s // 3)) % chips

    @pl.loop(0, chips)
    def _(s):
        @pl.when(s == 0)
        def _():
            ag_partner(0, cx)

        @pl.when(s == 1)
        def _():
            with jax.named_scope('q1'):
                ag_relays(4)
                ag_stage1(0)
                for cp_ in ag_own(1):
                    cp_.start()
                ag_stage2(0)
            with jax.named_scope('q1w'):
                for xc, h in ((xleft, 1), (xright, 0), (xfar, 0), (xfar, 1)):
                    ag_wait(4, xc, cc, h)
                for cp_ in wy_own:
                    cp_.start()
            ag_partner(0, xright)

        @pl.when(s == 2)
        def _():
            ag_partner(0, xleft)

        @pl.when(s == 3)
        def _():
            ag_stage3(0)
            ag_partner(0, xfar)

        r = pl.ds(chunk_of(s) * chunk, chunk)
        xc = xf[r, :]
        qf[r, :] = dot(xc, wqs[cc, 0], NN).astype(BF16)
        kv[r, :] = dot(xc, wkv[...], NN).astype(BF16)

    @pl.loop(0, chips)
    def _(s):
        @pl.when(s == 1)
        def _():
            with jax.named_scope('f1'):
                ag_stage1(1)
                for cp_ in ag_own(2):
                    cp_.start()

        @pl.when(s == 2)
        def _():
            with jax.named_scope('f2'):
                wy_pass()
                ag_stage2(1)

        i = chunk_of(s)
        r = pl.ds(i * chunk, chunk)
        row_id = lax.broadcasted_iota(jnp.int32, (chunk, seq), 0) + i * chunk
        keep = row_id >= lax.broadcasted_iota(jnp.int32, (chunk, seq), 1)
        for h in range(heads):
            hc = pl.ds(h * head_dim, head_dim)
            sc = dot(qf[r, hc], kv[:, 0:head_dim], NT) * scale
            sc = jnp.where(keep, sc, -jnp.inf)
            ex = jnp.exp(sc - jnp.max(sc, axis=-1, keepdims=True))
            pr = ex * (1.0 / jnp.sum(ex, axis=-1, keepdims=True))
            prob[h, r, :] = pr
            of[r, hc] = dot(pr.astype(BF16), kv[:, head_dim:], NN).astype(BF16)

    def mid_relays():
        ag_stage1(2)
        for cp_ in ag_own(5):
            cp_.start()

    with jax.named_scope('b0'):
        ag_stage3(1)
        ag_partner(1, cx)
        ag_partner(2, cx)

    @pl.loop(0, chips)
    def _(s):
        @pl.when(s == 1)
        def _():
            with jax.named_scope('b1'):
                for xc in (xright, xleft, xfar):
                    ag_partner(1, xc)
            with jax.named_scope('b1y'):
                y_first(0, 1)
                mid_relays()
                y_first(0, 0)
            with jax.named_scope('b1w'):
                ag_stage2(2)
                wy_end()
                ag_partner(2, xright)

        @pl.when(s == 2)
        def _():
            with jax.named_scope('b2'):
                ag_stage3(2)
                ag_partner(2, xleft)

        @pl.when(s == 3)
        def _():
            with jax.named_scope('b3'):
                ag_partner(2, xfar)

        with jax.named_scope('b_comp'):
            i = chunk_of(s)
            r = pl.ds(i * chunk, chunk)
            oc = of[r, :]
            do = dot(yf[r, :], wo[...], NT).astype(BF16)
            dof[r, :] = do
            od = do.astype(F32) * oc.astype(F32)
            for h in range(heads):
                hs = slice(h * head_dim, (h + 1) * head_dim)
                dp = dot(do[:, hs], kv[:, head_dim:], NT)
                ds = (prob[h, r, :] * (dp - jnp.sum(od[:, hs], axis=-1, keepdims=True))).astype(BF16)
                dsf[h, r, :] = ds
                dqf[r, hs] = (dot(ds, kv[:, 0:head_dim], NN) * scale).astype(BF16)

        @pl.when(s == 0)
        def _():
            dqa[0, cc] = dqf[own_rows, :]
            dq_copy(cx, cp).start()

        @pl.when(s > 0)
        def _():
            for core in range(2):
                dq_copy(i, core).start()

    y_first(1, 1)
    with jax.named_scope('t00_dkv'):
        for kc in range(chips):
            ks = slice(kc * chunk, (kc + 1) * chunk)
            qs = slice(kc * chunk, seq)
            dk = jnp.zeros((chunk, head_dim), F32)
            dv = jnp.zeros((chunk, head_dim), F32)
            for h in range(heads):
                hs = slice(h * head_dim, (h + 1) * head_dim)
                dk = dk + dot(dsf[h, qs, ks], qf[qs, hs], TN)
                dv = dv + dot(prob[h, qs, ks].astype(BF16), dof[qs, hs], TN)
            kvp[2 * kc:2 * kc + 2, :, 0:head_dim] = (dk * scale).reshape(2, tok, head_dim)
            kvp[2 * kc:2 * kc + 2, :, head_dim:] = dv.reshape(2, tok, head_dim)
        for xc in range(chips):
            kd_copy(xc).start()

    def kd_ring():
        kd_total.wait_recv()
        for xc in range(chips):
            blk = xc * 2 + cc
            kvp[blk] = kvp[blk] + kvr[xc]
        for kind in (1, 0):
            for side in range(2):
                k_copy(side, kind).start()

    with jax.named_scope('t00_y1'):
        y_first(1, 0)
        kd_ring()

    own = cx * 2 + cc

    cuts = (0, erow // 2, erow, erow + brow, width)

    def dx_near(j):
        cols = slice(cuts[j], cuts[j + 1])
        acc = dot(kvb[own_rows, :], wkv[cols, :], NT)
        for slot in (0, 1, chips - 1):
            for core in range(2):
                acc = acc + dot(dqa[slot, core], wqs[core, slot, cols, :], NT)
        return acc

    def dx_far(j, acc):
        cols = slice(cuts[j], cuts[j + 1])
        for core in range(2):
            acc = acc + dot(dqa[2, core], wqs[core, 2, cols, :], NT)
        dx_ref[:, cols] = acc.astype(BF16)

    def dx_part(j):
        dx_far(j, dx_near(j))

    def out_copy(k, src, dst):
        return pltpu.make_async_copy(src, dst, out_sem.at[k])

    outs = [out_copy(0, dx_ref, dx_out), out_copy(1, dwq_ref, dwq_out), out_copy(2, dwk_ref, dwk_out),
            out_copy(3, dwv_ref, dwv_out), out_copy(4, dwo_ref, dwo_out)]

    with jax.named_scope('t04_ag5'):
        ag_stage1(5)
    with jax.named_scope('t05_y0'):
        dw_blocks(0, 2)
        y_pass(0)
        dw_blocks(0, 3)
        dw_blocks(1, 2)
    with jax.named_scope('t06_ag5'):
        ag_stage2(5)
    with jax.named_scope('t07_kpass'):
        k_pass()
        for cp_ in ag_first(6):
            cp_.start()
    with jax.named_scope('t08_y1'):
        dw_blocks(1, 3)
        y_pass(1)
    with jax.named_scope('t09_ag5'):
        ag_stage3(5)
    with jax.named_scope('t10_kfin'):
        p = kr.at[:, pl.ds(0, 2)]
        rcopy(p, p, kr_s.at[0], kr_r.at[2], to_r).wait_recv()
        kvb[pl.ds(me * tok, half), :] = (kvp[own, 0:half, :] + kr[1, 0] + kr[0, 2]).astype(BF16)
        kvb[pl.ds(me * tok + half, half), :] = (kvp[own, half:, :] + kr[0, 0] + kr[1, 2]).astype(BF16)
        for cp_ in ag_own(3) + ag_second(6):
            cp_.start()
    with jax.named_scope('t11_dqw'):
        dq_total.wait_recv()
        wd_own.wait_recv()
        wd_rest.wait_recv()
    with jax.named_scope('t12_dxa'):
        dx_part(0)
    with jax.named_scope('t13_ag3'):
        ag_stage1(3)
        ag_stage1(6)
    with jax.named_scope('t14_dxa'):
        dx_part(1)
    with jax.named_scope('t15_ag3'):
        ag_stage2(3)
        ag_stage2(6)
    with jax.named_scope('t16_ag3'):
        ag_stage3(3)
        for xc in (cx, xright, xleft, xfar):
            ag_partner(3, xc)
    mrow = width // (2 * chips)
    krow = mrow // rows
    with jax.named_scope('t18_wk'):
        part = dot(xf[:, pl.ds(pl.multiple_of(me * mrow, mrow), mrow)], kvb[...], TN)
        wkp[...] = part.reshape(rows, krow, 2 * head_dim)

    def wk_copy(idx, blk, dev):
        return rcopy(wkp.at[blk], wkr.at[idx], wk_s.at[0], wk_r.at[0], dev)

    wk_total = rcopy(wkr, wkr, wk_s.at[0], wk_r.at[0], to_u)

    wk_copies = [wk_copy(0, yup, to_u), wk_copy(1, ydn, to_d), wk_copy(2, yfar, to_f)]
    for cp_ in wk_copies:
        cp_.start()
    with jax.named_scope('t19_dx2'):
        for xc in (cx, xright, xleft, xfar):
            ag_partner(5, xc)
        dx_part(2)
    with jax.named_scope('t19_ag6'):
        for xc in (cx, xright, xleft):
            ag_partner(6, xc)
        dxacc[...] = dx_near(3)
    with jax.named_scope('t19_ag6f'):
        ag_stage3(6)
    with jax.named_scope('t19_y0f'):
        first, second = y_final(0)
        dwo_ref[:, 0:wcol] = first
        dwo_ref[:, wcol:] = second
        outs[4].start()
    with jax.named_scope('t19_dx3'):
        ag_partner(6, xfar)
        dx_far(3, dxacc[...])
        outs[0].start()
    with jax.named_scope('t20_y1f'):
        for idx, val in enumerate(y_final(1)):
            val = val.T
            for h in range(heads):
                dwq_ref[pl.ds(idx * wcol * heads + h, wcol, stride=heads), :] = val[:, h * head_dim:(h + 1) * head_dim]
        outs[1].start()
    with jax.named_scope('t21_wkf'):
        wk_total.wait_recv()
        wk_sum = wkp[my] + wkr[0] + wkr[1] + wkr[2]
        dwk_ref[...] = wk_sum[:, 0:head_dim]
        dwv_ref[...] = wk_sum[:, head_dim:]
        outs[2].start()
        outs[3].start()

    with jax.named_scope('t22_sends'):
        for arr in range(7):
            ag_sent(arr)
        wd_own.wait_send()
        wd_rest.wait_send()
        wy_total(6).wait_send()
        dq_total.wait_send()
        kd_total.wait_send()
        rcopy(kvp.at[pl.ds(0, 3)], kvp.at[pl.ds(0, 3)], kr_s.at[0], kr_r.at[0], to_r).wait_send()
        rcopy(dwa.at[:, pl.ds(0, 6)], dwa.at[:, pl.ds(0, 6)], yr_s.at[0], yr_r.at[0, 0], to_u).wait_send()
        wk_total.wait_send()
        for cp_ in outs:
            cp_.wait()


def copy_out(*refs):
    n = (len(refs) - 1) // 2
    sem = refs[-1]
    copies = [pltpu.make_async_copy(refs[k], refs[n + k], sem.at[k]) for k in range(n)]
    for cp_ in copies:
        cp_.start()
    for cp_ in copies:
        cp_.wait()


VMEM_LIMIT = 60 * 1000 * 1000


def solution(mesh):
    model_size = mesh.shape['model']
    data_size = mesh.shape['data']
    tok_spec = P(('pod', 'data'), 'model', None)
    chips = model_size // 2

    def device_step(x_loc, dy_loc, w_q, w_k, w_v, w_o):
        tok, width = x_loc.shape[1:]
        head_dim = w_k.shape[2]
        head_cols = w_q.shape[1] * head_dim
        assert chips == 4 and data_size == 4 and w_k.shape[0] == 1 and x_loc.shape[0] == 1
        seq = model_size * tok
        half = tok // 2
        heads = head_cols // head_dim
        wcol = width // (2 * data_size)
        krow = width // (model_size * data_size)
        cfg = (tok, width, head_cols, head_dim, chips, data_size)
        vm = pltpu.VMEM
        dma = pltpu.SemaphoreType.DMA
        scratch = [
            vm((seq, width), BF16), vm((seq, width), BF16), vm((2, chips, width, head_cols), BF16), vm((head_cols, width), BF16),
            vm((width, 2 * head_dim), BF16), vm((heads * width, head_dim), BF16), vm((heads * width, head_dim), F32),
            vm((seq, head_cols), BF16), vm((seq, 2 * head_dim), BF16), vm((seq, head_cols), BF16),
            vm((heads, seq, seq), F32), vm((heads, seq, seq), BF16), vm((seq, head_cols), BF16), vm((seq, head_cols), BF16),
            vm((seq, 2 * head_dim), BF16), vm((chips, 2, tok, head_cols), BF16),
            vm((model_size, tok, 2 * head_dim), F32), vm((chips, tok, 2 * head_dim), F32), vm((2, 3, half, 2 * head_dim), F32),
            vm((2, 2 * data_size, head_cols, wcol), F32), vm((2, 2, 3, head_cols, wcol), F32),
            vm((data_size, krow, 2 * head_dim), F32), vm((3, krow, 2 * head_dim), F32),
            vm((tok, 3 * width // 16), F32), vm((tok, width), BF16), vm((heads * 2 * wcol, head_dim), F32), vm((krow, head_dim), F32), vm((krow, head_dim), F32),
            vm((head_cols, 2 * wcol), F32),
            dma((5,)), dma((5,)), dma((7,)), dma((7, 10)), dma((1,)), dma((3,)), dma((2,)), dma((2,)),
            dma((1,)), dma((1,)), dma((1,)), dma((1,)), dma((1,)), dma((3,)), dma((1,)), dma((2, 3)), dma((1,)), dma((1,)),
        ]
        anyspec = pl.BlockSpec(memory_space=pl.ANY)
        vspec = pl.BlockSpec(memory_space=pltpu.VMEM)
        shapes = (jax.ShapeDtypeStruct((tok, width), BF16), jax.ShapeDtypeStruct((heads * 2 * wcol, head_dim), F32),
                  jax.ShapeDtypeStruct((krow, head_dim), F32), jax.ShapeDtypeStruct((krow, head_dim), F32),
                  jax.ShapeDtypeStruct((head_cols, 2 * wcol), F32))
        outs = pl.pallas_call(
            functools.partial(body, cfg),
            out_shape=tuple(pltpu.VMEM(a.shape, a.dtype) for a in shapes),
            in_specs=[anyspec] * 6,
            out_specs=(anyspec,) * 5,
            scratch_shapes=scratch,
            compiler_params=pltpu.CompilerParams(collective_id=0, has_side_effects=True, vmem_limit_bytes=VMEM_LIMIT),
            name='attn_bwd',
        )(x_loc[0], dy_loc[0], w_q.reshape(width * heads, head_dim), w_o.reshape(head_cols, width), w_k[0], w_v[0])
        dx, dwq, dwk, dwv, dwo = pl.pallas_call(
            copy_out,
            out_shape=shapes,
            in_specs=[vspec] * 5,
            out_specs=(anyspec,) * 5,
            scratch_shapes=[dma((5,))],
            compiler_params=pltpu.CompilerParams(vmem_limit_bytes=4 * 1024 * 1024),
            name='copy_out',
        )(*outs)
        return (dx[None], dwq.reshape(2 * wcol, heads, head_dim), dwk, dwv, dwo.reshape(heads, head_dim, 2 * wcol))

    kv_rows = P(('pod', 'model', 'data'), None)
    return jax.shard_map(device_step, mesh=mesh,
                         in_specs=(tok_spec, tok_spec, P(None, 'model', None), P(), P(), P('model', None, None)),
                         out_specs=(tok_spec, P(('pod', 'data'), 'model', None), kv_rows, kv_rows, P(('pod', 'model'), None, 'data')),
                         check_vma=False)
```

profile of v0, /device:TPU:97, one launch (start us, length us, event | category | flops | bytes accessed | tf_op | source)
XLA Modules:
  0.0 86.2 jit_solution(5456567257887253983)
XLA Ops:
  0.6 84.2 %attn_bwd.1 = (bf16[128,2048]{1,0:T(8,128)(2,1)S(1)}, f32[1024,128]{1,0:T(8,128)S(1)}, f32[64,128]{1,0:T(8,128)S(1)}, f32[64,128]{1,0:T(8,128)S(1)}, f32[256,512]{1,0:T(8,128)S(1)}) custom-call(bf16[128,2048]{1,0:T(8,128)(2,1)} %bitcast.11, bf16[128,2048]{1,0:T(8,128)(2,1)} %bitcast.12, bf16[4096,128]{1,0:T(8,128)(2,1)} %bitcast.9, ...), custom_call_target="tpu_custom_call" | custom-call | tf_op jit(solution)/shard_map/attn_bwd/pallas_call | solution.py:627
  84.9 1.2 %copy_out.1 = (bf16[128,2048]{1,0:T(8,128)(2,1)}, f32[1024,128]{1,0:T(8,128)}, f32[64,128]{1,0:T(8,128)}, f32[64,128]{1,0:T(8,128)}, f32[256,512]{1,0:T(8,128)}) custom-call(bf16[128,2048]{1,0:T(8,128)(2,1)S(1)} %get-tuple-element.15.refs_0_, f32[1024,128]{1,0:T(8,128)S(1)} %get-tuple-element.16.refs_1_, f32[64,128]{1,0:T(8,128)S(1)} %get-tuple-element.17.refs_2_, ...), custom_call_target="tpu_custom_call" | custom-call | tf_op jit(solution)/shard_map/copy_out/pallas_call | solution.py:636
where the time goes:
time: 86.3 us; the launch traced here: 86.2 us
  Pallas kernels  85.4 us (99%)
    pallas_call x1, Pallas kernels, device_step(): pl.pallas_call(functools.partial(body, cfg), out_shape=tuple((pltpu.VMEM(...  84.2 us

commit v1 on v0

--- a/solution.py
+++ b/solution.py
@@ -31,7 +31,7 @@
     heads = head_cols // head_dim
     wcol = width // (2 * rows)
     hcol = width // 2
-    qrow = 5 * width // 32
+    qrow = width // 8
     erow = rows * qrow
     brow = (width - erow) // 2
     scale = head_dim ** -0.5
@@ -614,7 +614,7 @@
             vm((model_size, tok, 2 * head_dim), F32), vm((chips, tok, 2 * head_dim), F32), vm((2, 3, half, 2 * head_dim), F32),
             vm((2, 2 * data_size, head_cols, wcol), F32), vm((2, 2, 3, head_cols, wcol), F32),
             vm((data_size, krow, 2 * head_dim), F32), vm((3, krow, 2 * head_dim), F32),
-            vm((tok, 3 * width // 16), F32), vm((tok, width), BF16), vm((heads * 2 * wcol, head_dim), F32), vm((krow, head_dim), F32), vm((krow, head_dim), F32),
+            vm((tok, width // 4), F32), vm((tok, width), BF16), vm((heads * 2 * wcol, head_dim), F32), vm((krow, head_dim), F32), vm((krow, head_dim), F32),
             vm((head_cols, 2 * wcol), F32),
             dma((5,)), dma((5,)), dma((7,)), dma((7, 10)), dma((1,)), dma((3,)), dma((2,)), dma((2,)),
             dma((1,)), dma((1,)), dma((1,)), dma((1,)), dma((1,)), dma((3,)), dma((1,)), dma((2, 3)), dma((1,)), dma((1,)),

time: 86.3 us -> 85.3 us (0.988)
  Pallas kernels: 85.4 us -> 84.4 us
    pallas_call x1, Pallas kernels: 84.2 us -> 83.2 us  [device_step(): pl.pallas_call(functools.partial(body, cfg), out_shape=tuple((pltpu.VMEM(...]
where the time goes in v1:
time: 85.3 us; the launch traced here: 85.2 us
  Pallas kernels  84.4 us (99%)
    pallas_call x1, Pallas kernels, device_step(): pl.pallas_call(functools.partial(body, cfg), out_shape=tuple((pltpu.VMEM(...  83.2 us

profile of v1, /device:TPU:97, one launch (start us, length us, event | category | flops | bytes accessed | tf_op | source)
XLA Modules:
  0.0 85.2 jit_solution(16295572894042115516)
XLA Ops:
  0.6 83.2 %attn_bwd.1 = (bf16[128,2048]{1,0:T(8,128)(2,1)S(1)}, f32[1024,128]{1,0:T(8,128)S(1)}, f32[64,128]{1,0:T(8,128)S(1)}, f32[64,128]{1,0:T(8,128)S(1)}, f32[256,512]{1,0:T(8,128)S(1)}) custom-call(bf16[128,2048]{1,0:T(8,128)(2,1)} %bitcast.11, bf16[128,2048]{1,0:T(8,128)(2,1)} %bitcast.12, bf16[4096,128]{1,0:T(8,128)(2,1)} %bitcast.9, ...), custom_call_target="tpu_custom_call" | custom-call | tf_op jit(solution)/shard_map/attn_bwd/pallas_call | solution.py:627
  83.8 1.2 %copy_out.1 = (bf16[128,2048]{1,0:T(8,128)(2,1)}, f32[1024,128]{1,0:T(8,128)}, f32[64,128]{1,0:T(8,128)}, f32[64,128]{1,0:T(8,128)}, f32[256,512]{1,0:T(8,128)}) custom-call(bf16[128,2048]{1,0:T(8,128)(2,1)S(1)} %get-tuple-element.15.refs_0_, f32[1024,128]{1,0:T(8,128)S(1)} %get-tuple-element.16.refs_1_, f32[64,128]{1,0:T(8,128)S(1)} %get-tuple-element.17.refs_2_, ...), custom_call_target="tpu_custom_call" | custom-call | tf_op jit(solution)/shard_map/copy_out/pallas_call | solution.py:636
